TPU v7x, 32 devices: a whole 2x2x4 slice. The times are simulated.
32 devices in a mesh: ha: 8 (over z, core), wa: 2 (over y), ba: 2 (over x).
Axes of the slice: x: 2, y: 2, z: 4, core: 2. Of those that a mesh axis runs over, the one named last changes fastest.
Arguments:
- tokens: bfloat16 [2, 128, 64, 384], P('ba', 'ha', 'wa'), may hold values from -6 to 6
- cotangent: bfloat16 [2, 128, 64, 384], P('ba', 'ha', 'wa'), may hold values from -6 to 6
- w_qkv: bfloat16 [384, 1152], replicated, may hold values from -0.20412415 to 0.20412415
- w_proj: bfloat16 [384, 384], replicated, may hold values from -0.3125 to 0.3125
- table_logits: float32 [12, 225], replicated, may hold values from -6 to 6
- logit_scale: float32 [12], replicated, may hold values from 1 to 5.5
- gain: float32 [384], replicated, may hold values from 0.5 to 1.5
Outputs:
- d_tokens: bfloat16 [2, 128, 64, 384], P('ba', 'ha', 'wa')
- d_wqkv: float32 [384, 1152], P(None, 'ba')
- d_wproj: float32 [384, 384], P(None, 'ba')
- d_table: float32 [12, 225], replicated
- d_scale: float32 [12], replicated
- d_gain: float32 [384], replicated
All inputs are finite; a program needn't handle non-finite values.
Results may differ from a plain program's by a relative error of at most 0.01.
The roundings to bfloat16 on the way count: a program that leaves them out, or rounds other values in their place, can miss the bound.
Values may be sent and summed in bfloat16 or wider, within the bound.
A program may use at most 64 MiB of HBM per device.

v0:
```python
import math
import jax
import jax.numpy as jnp
from jax import lax
from jax.sharding import PartitionSpec as P

WIN = 8
EPS_NORM = 1e-05
MASK_FILL = -100.0
SCALE_CAP = math.log(100.0)
BIAS_RANGE = 16.0
HIGHEST = lax.Precision.HIGHEST


def from_behind(block, axis, distance):
    devices = range(lax.axis_size(axis))
    route = [((i - distance) % len(devices), i) for i in devices]
    return lax.ppermute(block, axis, route)


def coarse_product(form, left, right):
    return jnp.einsum(form, left, right, preferred_element_type=jnp.float32)


def fine_product(form, left, right):
    return jnp.einsum(form, left, right, precision=HIGHEST)


def to_windows(block, window):
    images, height, width, depth = block.shape
    tiles = block.reshape(images, height // window, window, width // window, window, depth)
    tiles = tiles.transpose(0, 1, 3, 2, 4, 5)
    return tiles.reshape(images, height // window * (width // window), window * window, depth)


def from_windows(tiles, images, height, width, window):
    depth = tiles.shape[-1]
    grid = tiles.reshape(images, height // window, width // window, window, window, depth)
    return grid.transpose(0, 1, 3, 2, 4, 5).reshape(images, height, width, depth)


def position_onehot(window):
    places = jnp.arange(window * window, dtype=jnp.int32)
    row_of = places // window
    col_of = places % window
    offset = (row_of[:, None] - row_of[None, :] + window - 1) * (2 * window - 1) + (
        col_of[:, None] - col_of[None, :] + window - 1
    )
    entries = jnp.arange((2 * window - 1) ** 2, dtype=jnp.int32)
    return (offset.reshape(-1)[:, None] == entries[None, :]).astype(jnp.float32)


def region_of(coords, extent, window):
    return (coords >= extent - window).astype(jnp.int32) + (coords >= extent - window // 2).astype(
        jnp.int32
    )


def region_mask(row_start, col_start, rows, cols, height, width, window):
    row_label = region_of(row_start + jnp.arange(rows, dtype=jnp.int32), height, window)
    col_label = region_of(col_start + jnp.arange(cols, dtype=jnp.int32), width, window)
    labels = row_label[:, None] * 3 + col_label[None, :]
    labels = labels.reshape(rows // window, window, cols // window, window).transpose(0, 2, 1, 3)
    labels = labels.reshape(-1, window * window)
    return jnp.where(labels[:, :, None] != labels[:, None, :], MASK_FILL, 0.0).astype(jnp.float32)


def grads_region(block, grad_block, row_start, col_start, height, width, window, params):
    w_qkv, w_proj, table_logits, logit_scale, gain = params
    images, rows, cols, depth = block.shape
    heads = logit_scale.shape[0]
    head_dim = depth // heads
    tiles = to_windows(block, window)
    grad_tiles = to_windows(grad_block, window)
    count = tiles.shape[1]
    length = window * window
    flat = tiles.reshape(-1, depth)
    qkv = jnp.dot(flat, w_qkv, preferred_element_type=jnp.float32).astype(jnp.bfloat16)
    qkv = qkv.reshape(images, count, length, 3, heads, head_dim)
    query = qkv[:, :, :, 0].astype(jnp.float32)
    keys = qkv[:, :, :, 1].astype(jnp.float32)
    values = qkv[:, :, :, 2]
    query_inv = lax.rsqrt(jnp.sum(query * query, -1, keepdims=True) + 1.0)
    key_inv = lax.rsqrt(jnp.sum(keys * keys, -1, keepdims=True) + 1.0)
    unit_query = query * query_inv
    unit_key = keys * key_inv
    scale = jnp.exp(jnp.minimum(logit_scale, SCALE_CAP))
    onehot = position_onehot(window)
    sigma = jax.nn.sigmoid(table_logits)
    rel_bias = jnp.dot(sigma * BIAS_RANGE, onehot.T, precision=HIGHEST).reshape(
        heads, length, length
    )
    mask = region_mask(row_start, col_start, rows, cols, height, width, window)
    cosine = fine_product("bnqhd,bnkhd->bnhqk", unit_query, unit_key)
    scores = scale[:, None, None] * cosine + rel_bias[None, None] + mask[None, :, None]
    top = jnp.max(scores, -1, keepdims=True)
    expo = jnp.exp(scores - top)
    probs = expo / jnp.sum(expo, -1, keepdims=True)
    probs_low = probs.astype(jnp.bfloat16)
    attended = (
        coarse_product("bnhqk,bnkhd->bnqhd", probs_low, values)
        .astype(jnp.bfloat16)
        .reshape(-1, depth)
    )
    proj = jnp.dot(attended, w_proj, preferred_element_type=jnp.float32)
    centre = proj - jnp.mean(proj, -1, keepdims=True)
    inv_std = lax.rsqrt(jnp.mean(centre * centre, -1, keepdims=True) + EPS_NORM)
    normed = centre * inv_std
    upstream = grad_tiles.reshape(-1, depth).astype(jnp.float32)
    d_gain = jnp.sum(upstream * normed, 0)
    scaled = upstream * gain
    d_proj = inv_std * (
        scaled
        - jnp.mean(scaled, -1, keepdims=True)
        - normed * jnp.mean(scaled * normed, -1, keepdims=True)
    )
    d_proj = d_proj.astype(jnp.bfloat16)
    d_wproj = jnp.dot(attended.T, d_proj, preferred_element_type=jnp.float32)
    d_att = jnp.dot(d_proj, w_proj.T, preferred_element_type=jnp.float32).astype(jnp.bfloat16)
    d_att = d_att.reshape(images, count, length, heads, head_dim)
    d_probs = coarse_product("bnqhd,bnkhd->bnhqk", d_att, values)
    d_values = coarse_product("bnhqk,bnqhd->bnkhd", probs_low, d_att)
    d_scores = probs * (d_probs - jnp.sum(d_probs * probs, -1, keepdims=True))
    d_bias = jnp.sum(d_scores, (0, 1)).reshape(heads, length * length)
    d_table = jnp.dot(d_bias, onehot, precision=HIGHEST) * (BIAS_RANGE * sigma * (1.0 - sigma))
    live = (logit_scale < SCALE_CAP).astype(jnp.float32)
    d_scale = jnp.sum(d_scores * cosine, (0, 1, 3, 4)) * scale * live
    d_cos = d_scores * scale[:, None, None]
    d_unit_q = fine_product("bnhqk,bnkhd->bnqhd", d_cos, unit_key)
    d_unit_k = fine_product("bnhqk,bnqhd->bnkhd", d_cos, unit_query)
    d_query = query_inv * (
        d_unit_q - unit_query * jnp.sum(unit_query * d_unit_q, -1, keepdims=True)
    )
    d_key = key_inv * (d_unit_k - unit_key * jnp.sum(unit_key * d_unit_k, -1, keepdims=True))
    d_qkv = jnp.stack([d_query, d_key, d_values], 3).astype(jnp.bfloat16).reshape(-1, 3 * depth)
    d_wqkv = jnp.dot(flat.T, d_qkv, preferred_element_type=jnp.float32)
    d_flat = jnp.dot(d_qkv, w_qkv.T, preferred_element_type=jnp.float32).astype(jnp.bfloat16)
    d_block = from_windows(d_flat.reshape(images, count, length, depth), images, rows, cols, window)
    return (d_block, (d_wqkv, d_wproj, d_table, d_scale, d_gain))


def shift_in(tokens, cotangent, shift):
    stacked = jnp.stack([tokens, cotangent])
    below = from_behind(stacked[:, :, :shift], "ha", -1)
    tall = jnp.concatenate([stacked[:, :, shift:], below], 2)
    beside = from_behind(tall[:, :, :, :shift], "wa", -1)
    moved = jnp.concatenate([tall[:, :, :, shift:], beside], 3)
    return (moved[0], moved[1])


def shift_out(grads, shift):
    rows = grads.shape[1]
    cols = grads.shape[2]
    right = from_behind(grads[:, :, cols - shift :], "wa", 1)
    wide = jnp.concatenate([right, grads[:, :, : cols - shift]], 2)
    lower = from_behind(wide[:, rows - shift :], "ha", 1)
    return jnp.concatenate([lower, wide[:, : rows - shift]], 1)


def shards(tokens, cotangent, w_qkv, w_proj, table_logits, logit_scale, gain):
    rows = tokens.shape[1]
    cols = tokens.shape[2]
    shift = WIN // 2
    height = rows * lax.axis_size("ha")
    width = cols * lax.axis_size("wa")
    row_base = lax.axis_index("ha") * rows
    col_base = lax.axis_index("wa") * cols
    params = (w_qkv, w_proj, table_logits, logit_scale, gain)
    moved, moved_grad = shift_in(tokens, cotangent, shift)
    d_moved, parts = grads_region(moved, moved_grad, row_base, col_base, height, width, WIN, params)
    back = shift_out(d_moved, shift)
    d_tokens = (cotangent.astype(jnp.float32) + back.astype(jnp.float32)).astype(jnp.bfloat16)
    d_wqkv, d_wproj, d_table, d_scale, d_gain = parts
    half_qkv, half_proj = (
        lax.psum_scatter(d_wqkv.astype(jnp.bfloat16), "ba", scatter_dimension=1, tiled=True).astype(
            jnp.float32
        ),
        lax.psum_scatter(
            d_wproj.astype(jnp.bfloat16), "ba", scatter_dimension=1, tiled=True
        ).astype(jnp.float32),
    )
    half_qkv, half_proj = lax.psum((half_qkv, half_proj), ("ha", "wa"))
    d_table, d_scale, d_gain = lax.psum((d_table, d_scale, d_gain), ("ha", "wa", "ba"))
    return (d_tokens, half_qkv, half_proj, d_table, d_scale, d_gain)


def solution(mesh):
    return jax.shard_map(
        shards,
        mesh=mesh,
        in_specs=(P("ba", "ha", "wa", None), P("ba", "ha", "wa", None), P(), P(), P(), P(), P()),
        out_specs=(P("ba", "ha", "wa", None), P(None, "ba"), P(None, "ba"), P(), P(), P()),
        check_vma=False,
    )
```

profile of v0, /device:TPU:0, one launch (start us, length us, event | category | flops | bytes accessed | tf_op | source)
XLA Modules:
  0.0 213.7 jit_solution(15621993046436900654)
XLA Ops:
  7.2 1.0 pad_maximum_fusion.2
  8.3 4.6 %collective-permute-start = (bf16[2,1,4,32,384]{4,3,2,1,0:T(8,128)(2,1)S(1)}, bf16[2,1,4,32,384]{4,3,2,1,0:T(8,128)(2,1)S(1)}, u32[]{:S(2)}, u32[]{:S(2)}) collective-permute-start(bf16[2,1,4,32,384]{4,3,2,1,0:T(8,128)(2,1)S(1)} %pad_maximum_fusion.2), channel_id=1, source_target_pairs={{4,0},{8,4},{12,8},{16,12},{20,16},{24,20},{28,24},{0,28},{5,1},{9... | collective-permute-start | bytes 589832 | tf_op jit(solution)/shard_map/ppermute | solution.py:18
  12.8 1.1 fusion.52
  14.2 0.8 compare_select_fusion
  15.2 2.0 fusion.2
  17.4 0.9 copy.85
  18.3 1.6 collective-permute-start.1
  20.2 2.8 %collective-permute-done.1 = bf16[2,1,16,4,384]{4,3,2,1,0:T(4,128)(2,1)S(1)} collective-permute-done((bf16[2,1,16,4,384]{4,3,2,1,0:T(4,128)(2,1)S(1)}, bf16[2,1,16,4,384]{4,3,2,1,0:T(4,128)(2,1)S(1)}, u32[]{:S(2)}, u32[]{:S(2)}) %collective-permute-start.1) | collective-permute-done | bytes 98336 | tf_op jit(solution)/shard_map/ppermute | solution.py:18
  23.0 0.9 fusion.57
  24.0 0.7 copy-done.9
  24.7 0.8 convolution_convert_fusion
  25.5 0.6 copy.82
  26.1 3.0 %reshape.449 = bf16[1,8,64,3,12,32]{2,1,5,4,3,0:T(8,128)(2,1)} reshape(bf16[512,1152]{0,1:T(8,128)(2,1)S(1)} %copy.82) | data formatting | bytes 2359296 | tf_op jit(solution)/shard_map/reshape | solution.py:79
  29.2 1.8 fusion.67
  31.7 5.2 %fusion.29 = f32[8,12,64,64]{2,3,1,0:T(8,128)S(1)} fusion(f32[8,64,12]{1,2,0:T(8,128)S(1)} %add_rsqrt_fusion.1, f32[8,64,12]{1,2,0:T(8,128)S(1)} %add_rsqrt_fusion, bf16[1,8,64,1,12,32]{2,1,5,4,3,0:T(8,128)(2,1)S(1)} %get-tuple-element.16, bf16[1,8,64,1,12,32]{2,1,5,4,3,0:T(8,128)(2,1)S(1)} %get-tuple-element.17), kind=kOutput, calls=%fused_computation.41 | convolution fusion | flops 151781376 | bytes 2408448 | tf_op jit(solution)/shard_map/bnqhd,bnkhd->bnhqk/dot_general | solution.py:26
  36.9 1.2 fusion.68
  38.2 0.5 copy-done.1
  38.6 0.5 fusion.40
  39.2 1.1 copy-done.3
  40.3 0.5 copy.88
  40.8 1.3 reshape.451
  42.1 1.6 fusion.69
  43.9 0.9 copy.89
  44.8 2.3 %copy.90 = f32[512,384]{0,1:T(8,128)} copy(f32[512,384]{1,0:T(8,128)} %bitcast.140) | data formatting | bytes 1572864 | tf_op jit(solution)/shard_map/convert_element_type | solution.py:109
  47.1 1.2 fusion.42
  48.3 1.4 multiply_reduce_fusion.2
  49.8 1.4 multiply_convert_fusion
  51.7 1.1 convolution_convert_fusion.5
  53.0 1.3 reshape.452
  54.3 3.6 %multiply_reduce_fusion.1 = (f32[8,12,64]{2,1,0:T(8,128)S(1)}, f32[8,12,64,64]{2,3,1,0:T(8,128)S(1)}) fusion(f32[8,12,64,64]{2,3,1,0:T(8,128)} %copy-done.3, f32[8,12,64]{2,1,0:T(8,128)S(1)} %get-tuple-element.21, bf16[1,8,64,1,12,32]{2,1,5,4,3,0:T(8,128)(2,1)} %copy-done.14, bf16[8,64,12,32]{1,0,3,2:T(8,128)(2,1)} %reshape.452), kind=kOutput, calls=%fused_computation.7 | convolution fusion | flops 26339328 | bytes 3981312 | tf_op jit(solution)/shard_map/bnqhd,bnkhd->bnhqk/dot_general | solution.py:22
  57.9 0.6 copy-done.4
  58.6 2.2 %multiply_reduce_fusion = (f32[12]{0:T(128)S(1)}, f32[12,64,64]{1,2,0:T(8,128)}, f32[8,12,64,64]{2,3,1,0:T(8,128)S(1)}) fusion(f32[8,12,64,64]{2,3,1,0:T(8,128)S(1)} %copy-done.2, f32[8,12,64,64]{2,3,1,0:T(8,128)S(1)} %get-tuple-element.26, f32[8,12,64]{2,1,0:T(8,128)S(1)} %get-tuple-element.25, f32[8,12,64,64]{2,3,1,0:T(8,128)S(1)} %copy-done.4, ...), kind=kLoop, calls=%fused_computation.5 | loop fusion | flops 2310132 | bytes 6537264 | tf_op jit(solution)/shard_map/reduce_sum | solution.py:127
  60.7 4.3 %fusion.22 = (f32[8,64,12]{1,2,0:T(8,128)S(1)}, f32[8,12,32,64]{3,2,1,0:T(8,128)}) fusion(f32[8,64,12]{1,2,0:T(8,128)S(1)} %add_rsqrt_fusion.1, bf16[1,8,64,1,12,32]{2,1,5,4,3,0:T(8,128)(2,1)S(1)} %get-tuple-element.17, f32[8,12,64,64]{2,3,1,0:T(8,128)S(1)} %get-tuple-element.15, f32[12]{0:T(128)S(1)} %minimum_exponential_fusion, ...), kind=kOutput, calls=%fused_computation.35 | convolution fusion | flops 152561664 | bytes 3219504 | tf_op jit(solution)/shard_map/bnhqk,bnkhd->bnqhd/dot_general | solution.py:26
  65.0 6.8 %fusion.18 = (f32[8,64,12]{1,2,0:T(8,128)}, f32[8,12,32,64]{3,2,1,0:T(8,128)}) fusion(f32[8,64,12]{1,2,0:T(8,128)S(1)} %add_rsqrt_fusion, bf16[1,8,64,1,12,32]{2,1,5,4,3,0:T(8,128)(2,1)S(1)} %get-tuple-element.16, f32[8,12,64,64]{2,3,1,0:T(8,128)S(1)} %get-tuple-element.15, f32[12]{0:T(128)S(1)} %minimum_exponential_fusion, ...), kind=kOutput, calls=%fused_computation.31 | convolution fusion | flops 152561664 | bytes 3219504 | tf_op jit(solution)/shard_map/bnhqk,bnqhd->bnkhd/dot_general | solution.py:26
  71.9 0.9 convolution_bitcast_fusion
  73.1 2.6 %fusion.21 = (bf16[1,8,64,1,12,32]{2,5,4,1,3,0:T(8,128)(2,1)S(1)}, bf16[1,8,64,1,12,32]{2,5,4,1,3,0:T(8,128)(2,1)S(1)}) fusion(f32[8,12,32,64]{3,2,1,0:T(8,128)} %get-tuple-element.28, f32[8,64,12]{1,2,0:T(8,128)} %get-tuple-element.27, f32[8,64,12]{1,2,0:T(8,128)S(1)} %add_rsqrt_fusion, bf16[1,8,64,1,12,32]{2,1,5,4,3,0:T(8,128)(2,1)S(1)} %get-tuple-element.16, ...), kind=kLoop, calls=%fused_computation.34 | loop fusion | flops 2359296 | bytes 3244032 | tf_op jit(solution)/shard_map/stack | solution.py:135
  75.7 0.6 maximum_convert_fusion
  76.3 2.7 %copy.98 = bf16[1,8,64,3,12,32]{2,1,5,4,3,0:T(8,128)(2,1)S(1)} copy(bf16[1,8,64,3,12,32]{2,5,4,1,3,0:T(8,128)(2,1)S(1)} %maximum_convert_fusion) | data formatting | bytes 2359296 | tf_op jit(solution)/shard_map/convert_element_type | solution.py:135
  79.1 2.4 %convert_element_type.207 = bf16[512,1152]{0,1:T(8,128)(2,1)} reshape(bf16[1,8,64,3,12,32]{2,1,5,4,3,0:T(8,128)(2,1)S(1)} %copy.98) | data formatting | bytes 2359296 | tf_op jit(solution)/shard_map/convert_element_type | solution.py:135
  81.5 3.1 %convolution_convert_fusion.1 = bf16[384,1152]{0,1:T(8,128)(2,1)} fusion(bf16[512,1152]{0,1:T(8,128)(2,1)} %convert_element_type.207, bf16[512,384]{1,0:T(8,128)(2,1)} %bitcast.142), kind=kOutput, calls=%fused_computation.15 | convolution fusion | flops 453427200 | bytes 2457600 | tf_op jit(solution)/shard_map/dot_general | solution.py:136
  84.9 0.9 copy-done.11
  85.8 0.9 convolution_convert_fusion.3
  86.8 1.6 collective-permute-start.2
  88.4 1.4 fusion.41
  89.8 1.1 collective-permute-done.2
  91.1 39.5 %all-reduce = (f32[12,225]{1,0:T(8,128)}, f32[12]{0:T(128)}, f32[384]{0:T(512)}) all-reduce(f32[12,225]{1,0:T(8,128)S(1)} %fusion.41, f32[12]{0:T(128)S(1)} %compare_select_fusion.1, f32[384]{0:T(512)S(1)} %get-tuple-element.8), channel_id=1, replica_groups=mesh['ha'=8,'wa'=2,'ba'=2] {'ha','wa','ba'}, use_global_device_ids=true, to_apply=%region_16.17 | all-reduce | flops 3096 | bytes 24768 | tf_op jit(solution)/shard_map/psum | solution.py:183
  130.6 0.9 add_convert_fusion
  131.5 75.2 %all-reduce.3 = (f32[384,576]{0,1:T(8,128)}, f32[384,192]{0,1:T(8,128)}) all-reduce(bf16[384,576]{0,1:T(8,128)(2,1)} %reduce-scatter.3.cloned.1.call-done, bf16[384,192]{0,1:T(8,128)(2,1)} %reduce-scatter.5.cloned.1.call-done), channel_id=1, replica_groups=mesh['ha'=8,'wa'=2,'ba'=2] {'ha','wa'}, use_global_device_ids=true, to_apply=%region_12.13 | all-reduce | flops 294912 | bytes 1769472 | tf_op jit(solution)/shard_map/psum | solution.py:182
  (75 shorter events, 3.4 us)
Async XLA Ops:
  7.2 17.5 %copy-start = (bf16[384,1152]{1,0:T(8,128)(2,1)S(1)}, bf16[384,1152]{1,0:T(8,128)(2,1)}, u32[]{:S(2)}) copy-start(bf16[384,1152]{1,0:T(8,128)(2,1)} %param.9) | copy-start | bytes 2654212
  7.2 8.0 %copy-start.17 = (f32[12,225]{1,0:T(8,128)S(1)}, f32[12,225]{1,0:T(8,128)}, u32[]{:S(2)}) copy-start(f32[12,225]{1,0:T(8,128)} %param.11) | copy-start | bytes 32404
  7.2 124.3 %reduce-scatter.5.cloned.1.call-start = ((), (), s32[]{:S(2)}) async-start(), calls=%async_computation.3 | async-start | bytes 442368 | tf_op jit(solution)/shard_map/reduce_scatter | solution.py:178
  8.3 10.0 %collective-permute-start = (bf16[2,1,4,32,384]{4,3,2,1,0:T(8,128)(2,1)S(1)}, bf16[2,1,4,32,384]{4,3,2,1,0:T(8,128)(2,1)S(1)}, u32[]{:S(2)}, u32[]{:S(2)}) collective-permute-start(bf16[2,1,4,32,384]{4,3,2,1,0:T(8,128)(2,1)S(1)} %pad_maximum_fusion.2), channel_id=1, source_target_pairs={{4,0},{8,4},{12,8},{16,12},{20,16},{24,20},{28,24},{0,28},{5,1},{9... | collective-permute-start | bytes 589832 | tf_op jit(solution)/shard_map/ppermute | solution.py:18
  14.0 4.3 %copy-start.18 = (f32[12]{0:T(128)S(1)}, f32[12]{0:T(128)}, u32[]{:S(2)}) copy-start(f32[12]{0:T(128)} %param.12) | copy-start | bytes 148
  18.3 4.7 %collective-permute-start.1 = (bf16[2,1,16,4,384]{4,3,2,1,0:T(4,128)(2,1)S(1)}, bf16[2,1,16,4,384]{4,3,2,1,0:T(4,128)(2,1)S(1)}, u32[]{:S(2)}, u32[]{:S(2)}) collective-permute-start(bf16[2,1,16,4,384]{4,3,2,1,0:T(4,128)(2,1)S(1)} %pad_maximum_fusion.4), channel_id=1, source_target_pairs={{2,0},{0,2},{3,1},{1,3},{6,4},{4,6},{7,5},{5,7},{10,8},{8,10},{11,... | collective-permute-start | bytes 294920 | tf_op jit(solution)/shard_map/ppermute | solution.py:18
  24.0 0.7 copy-start.9
  30.9 7.7 %copy-start.14 = (bf16[1,8,64,1,12,32]{2,1,5,4,3,0:T(8,128)(2,1)}, bf16[1,8,64,1,12,32]{2,1,5,4,3,0:T(8,128)(2,1)S(1)}, u32[]{:S(2)}) copy-start(bf16[1,8,64,1,12,32]{2,1,5,4,3,0:T(8,128)(2,1)S(1)} %get-tuple-element.18) | copy-start | bytes 1179652
  31.7 5.2 %copy-start.10 = (f32[12,64,64]{1,2,0:T(8,128)S(1)}, f32[12,64,64]{1,2,0:T(8,128)}, u32[]{:S(2)}) copy-start(f32[12,64,64]{1,2,0:T(8,128)} %copy.85) | copy-start | bytes 589828
  31.7 5.2 %copy-start.13 = (f32[8,64,64]{1,2,0:T(8,128)S(1)}, f32[8,64,64]{1,2,0:T(8,128)}, u32[]{:S(2)}) copy-start(f32[8,64,64]{1,2,0:T(8,128)} %compare_select_fusion) | copy-start | bytes 393220
  36.9 1.7 copy-start.1
  38.6 1.7 copy-start.3
  42.1 1.7 copy-start.6
  43.9 3.2 %copy-start.16 = (f32[384]{0:T(512)S(1)}, f32[384]{0:T(512)}, u32[]{:S(2)}) copy-start(f32[384]{0:T(512)} %param.13) | copy-start | bytes 4612
  49.8 1.4 copy-start.12
  49.8 1.9 copy-start.5
  54.3 3.6 %copy-start.2 = (f32[8,12,64,64]{2,3,1,0:T(8,128)S(1)}, f32[8,12,64,64]{2,3,1,0:T(8,128)}, u32[]{:S(2)}) copy-start(f32[8,12,64,64]{2,3,1,0:T(8,128)} %copy-done.1) | copy-start | bytes 4718596
  54.3 4.3 %copy-start.4 = (f32[8,12,64,64]{2,3,1,0:T(8,128)S(1)}, f32[8,12,64,64]{2,3,1,0:T(8,128)}, u32[]{:S(2)}) copy-start(f32[8,12,64,64]{2,3,1,0:T(8,128)} %copy-done.3) | copy-start | bytes 4718596
  65.0 6.8 %copy-start.15 = (bf16[8,64,12,32]{1,0,3,2:T(8,128)(2,1)S(1)}, bf16[8,64,12,32]{1,0,3,2:T(8,128)(2,1)}, u32[]{:S(2)}) copy-start(bf16[8,64,12,32]{1,0,3,2:T(8,128)(2,1)} %reshape.452) | copy-start | bytes 1179652
  72.8 58.7 %reduce-scatter.3.cloned.1.call-start = ((), (), s32[]{:S(2)}) async-start(), calls=%async_computation.2 | async-start | bytes 1327104 | tf_op jit(solution)/shard_map/reduce_scatter | solution.py:175
  81.5 3.1 %copy-start.8 = (f32[12,64,64]{1,2,0:T(8,128)S(1)}, f32[12,64,64]{1,2,0:T(8,128)}, u32[]{:S(2)}) copy-start(f32[12,64,64]{1,2,0:T(8,128)} %get-tuple-element.7) | copy-start | bytes 589828
  84.6 1.3 copy-start.11
  86.7 43.9 %copy-start.7 = (bf16[1,16,32,384]{3,2,1,0:T(8,128)(2,1)S(1)}, bf16[1,16,32,384]{3,2,1,0:T(8,128)(2,1)}, u32[]{:S(2)}) copy-start(bf16[1,16,32,384]{3,2,1,0:T(8,128)(2,1)} %param.8) | copy-start | bytes 1179652
  86.8 4.2 %collective-permute-start.2 = (bf16[1,16,4,384]{3,2,1,0:T(4,128)(2,1)S(1)}, bf16[1,16,4,384]{3,2,1,0:T(4,128)(2,1)S(1)}, u32[]{:S(2)}, u32[]{:S(2)}) collective-permute-start(bf16[1,16,4,384]{3,2,1,0:T(4,128)(2,1)S(1)} %slice.61), channel_id=1, source_target_pairs={{2,0},{0,2},{3,1},{1,3},{6,4},{4,6},{7,5},{5,7},{10,8},{8,10},{11,... | collective-permute-start | bytes 147464 | tf_op jit(solution)/shard_map/ppermute | solution.py:18
  91.0 39.6 %collective-permute-start.3 = (bf16[1,4,32,384]{3,2,1,0:T(8,128)(2,1)S(1)}, bf16[1,4,32,384]{3,2,1,0:T(8,128)(2,1)S(1)}, u32[]{:S(2)}, u32[]{:S(2)}) collective-permute-start(bf16[1,4,32,384]{3,2,1,0:T(8,128)(2,1)S(1)} %pad_maximum_fusion.3), channel_id=1, source_target_pairs={{28,0},{0,4},{4,8},{8,12},{12,16},{16,20},{20,24},{24,28},{29,1},{... | collective-permute-start | bytes 294920 | tf_op jit(solution)/shard_map/ppermute | solution.py:18
Sparse Core Ops, SparseCore 0:
  73.0 11.1 reduce-scatter.4
  87.0 19.1 reduce-scatter.2
where the time goes:
time: 218 us; the launch traced here: 214 us
  blocking collectives  115 us (53%)
  matrix products  32.7 us (15%)
  local copies, waits for them, and re-layouts  22.7 us (10%)
  other arithmetic  16.8 us (8%)
  between operations  14.7 us (7%)
  starting transfers between devices  8.08 us (4%)
  waiting for transfers between devices  4.03 us (2%)
    psum x1, blocking collectives, shards(): half_qkv, half_proj = lax.psum((half_qkv, half_proj), ('ha', 'wa'))  75.2 us
    psum x1, blocking collectives, shards(): lax.psum((d_table, d_scale, d_gain), ('ha', 'wa', 'ba'))  39.5 us
    dot_general x3, matrix products, fine_product(): return jnp.einsum(form, left, right, precision=HIGHEST)  16.3 us
    ppermute x4, starting transfers between devices, from_behind(): return lax.ppermute(block, axis, route)  7.79 us
    convert_element_type x2, local copies, waits for them, and re-layouts, grads_region(): jnp.stack([d_query, d_key, d_values], 3).astype(jnp.bfloat16)  5.15 us
    dot_general x3, matrix products, coarse_product(): return jnp.einsum(form, left, right, preferred_element_type=jnp.float32)  5.11 us
  transfers between devices with their start and end apart: 6, of which 2 were waited for; matrix products, arithmetic and copies ran while one was open for 10% of the time, Pallas kernels for 0%

commit v1 on v0

--- a/solution.py
+++ b/solution.py
@@ -180,7 +180,7 @@
         ).astype(jnp.float32),
     )
     half_qkv, half_proj = lax.psum((half_qkv, half_proj), ("ha", "wa"))
-    d_table, d_scale, d_gain = lax.psum((d_table, d_scale, d_gain), ("ha", "wa", "ba"))
+    d_table, d_scale, d_gain = lax.psum(lax.psum((d_table, d_scale, d_gain), "ha"), ("wa", "ba"))
     return (d_tokens, half_qkv, half_proj, d_table, d_scale, d_gain)
 
 

time: 218 us -> 225 us (1.032)
  blocking collectives: 115 us -> 121 us
    psum x1 -> x2, blocking collectives: 39.5 us -> 46.3 us  [the longest x1 29.3 us: shards(): lax.psum((d_table, d_scale, d_gain), 'ha')]
  transfers between devices with their start and end apart: 6 -> 6, of which waited for: 2 -> 2; matrix products, arithmetic and copies ran while one was open for 10% -> 9% of each run, Pallas kernels for 0% -> 0%
where the time goes in v1:
time: 225 us; the launch traced here: 220 us
  blocking collectives  121 us (54%)
  matrix products  32.7 us (15%)
  local copies, waits for them, and re-layouts  22.7 us (10%)
  other arithmetic  16.8 us (7%)
  between operations  14.7 us (7%)
  starting transfers between devices  8.08 us (4%)
  waiting for transfers between devices  4.03 us (2%)
    psum x1, blocking collectives, shards(): half_qkv, half_proj = lax.psum((half_qkv, half_proj), ('ha', 'wa'))  75.2 us
    psum x1, blocking collectives, shards(): lax.psum((d_table, d_scale, d_gain), 'ha')  29.3 us
    psum x1, blocking collectives, shards(): lax.psum(lax.psum((d_table, d_scale, d_gain), 'ha'), ('wa', 'ba'))  17 us
    dot_general x3, matrix products, fine_product(): return jnp.einsum(form, left, right, precision=HIGHEST)  16.3 us
    ppermute x4, starting transfers between devices, from_behind(): return lax.ppermute(block, axis, route)  7.79 us
    convert_element_type x2, local copies, waits for them, and re-layouts, grads_region(): jnp.stack([d_query, d_key, d_values], 3).astype(jnp.bfloat16)  5.15 us
    dot_general x3, matrix products, coarse_product(): return jnp.einsum(form, left, right, preferred_element_type=jnp.float32)  5.11 us
  transfers between devices with their start and end apart: 6, of which 2 were waited for; matrix products, arithmetic and copies ran while one was open for 9% of the time, Pallas kernels for 0%

profile of v1, /device:TPU:0, one launch (start us, length us, event | category | flops | bytes accessed | tf_op | source)
XLA Modules:
  0.0 220.5 jit_solution(2683566608960653848)
XLA Ops:
  7.2 1.0 pad_maximum_fusion.2
  8.3 4.6 %collective-permute-start = (bf16[2,1,4,32,384]{4,3,2,1,0:T(8,128)(2,1)S(1)}, bf16[2,1,4,32,384]{4,3,2,1,0:T(8,128)(2,1)S(1)}, u32[]{:S(2)}, u32[]{:S(2)}) collective-permute-start(bf16[2,1,4,32,384]{4,3,2,1,0:T(8,128)(2,1)S(1)} %pad_maximum_fusion.2), channel_id=1, source_target_pairs={{4,0},{8,4},{12,8},{16,12},{20,16},{24,20},{28,24},{0,28},{5,1},{9... | collective-permute-start | bytes 589832 | tf_op jit(solution)/shard_map/ppermute | solution.py:18
  12.8 1.1 fusion.52
  14.2 0.8 compare_select_fusion
  15.2 2.0 fusion.2
  17.4 0.9 copy.85
  18.3 1.6 collective-permute-start.1
  20.2 2.8 %collective-permute-done.1 = bf16[2,1,16,4,384]{4,3,2,1,0:T(4,128)(2,1)S(1)} collective-permute-done((bf16[2,1,16,4,384]{4,3,2,1,0:T(4,128)(2,1)S(1)}, bf16[2,1,16,4,384]{4,3,2,1,0:T(4,128)(2,1)S(1)}, u32[]{:S(2)}, u32[]{:S(2)}) %collective-permute-start.1) | collective-permute-done | bytes 98336 | tf_op jit(solution)/shard_map/ppermute | solution.py:18
  23.0 0.9 fusion.57
  24.0 0.7 copy-done.9
  24.7 0.8 convolution_convert_fusion
  25.5 0.6 copy.82
  26.1 3.0 %reshape.449 = bf16[1,8,64,3,12,32]{2,1,5,4,3,0:T(8,128)(2,1)} reshape(bf16[512,1152]{0,1:T(8,128)(2,1)S(1)} %copy.82) | data formatting | bytes 2359296 | tf_op jit(solution)/shard_map/reshape | solution.py:79
  29.2 1.8 fusion.67
  31.7 5.2 %fusion.29 = f32[8,12,64,64]{2,3,1,0:T(8,128)S(1)} fusion(f32[8,64,12]{1,2,0:T(8,128)S(1)} %add_rsqrt_fusion.1, f32[8,64,12]{1,2,0:T(8,128)S(1)} %add_rsqrt_fusion, bf16[1,8,64,1,12,32]{2,1,5,4,3,0:T(8,128)(2,1)S(1)} %get-tuple-element.19, bf16[1,8,64,1,12,32]{2,1,5,4,3,0:T(8,128)(2,1)S(1)} %get-tuple-element.20), kind=kOutput, calls=%fused_computation.41 | convolution fusion | flops 151781376 | bytes 2408448 | tf_op jit(solution)/shard_map/bnqhd,bnkhd->bnhqk/dot_general | solution.py:26
  36.9 1.2 fusion.68
  38.6 0.5 fusion.40
  39.2 1.1 copy-done.3
  40.3 0.5 copy.88
  40.8 1.3 reshape.451
  42.1 1.6 fusion.69
  43.9 0.9 copy.89
  44.8 2.3 %copy.90 = f32[512,384]{0,1:T(8,128)} copy(f32[512,384]{1,0:T(8,128)} %bitcast.140) | data formatting | bytes 1572864 | tf_op jit(solution)/shard_map/convert_element_type | solution.py:109
  47.1 1.2 fusion.42
  48.3 1.4 multiply_reduce_fusion.2
  49.8 1.4 multiply_convert_fusion
  51.7 1.1 convolution_convert_fusion.5
  53.0 1.3 reshape.452
  54.3 3.6 %multiply_reduce_fusion.1 = (f32[8,12,64]{2,1,0:T(8,128)S(1)}, f32[8,12,64,64]{2,3,1,0:T(8,128)S(1)}) fusion(f32[8,12,64,64]{2,3,1,0:T(8,128)} %copy-done.3, f32[8,12,64]{2,1,0:T(8,128)S(1)} %get-tuple-element.24, bf16[1,8,64,1,12,32]{2,1,5,4,3,0:T(8,128)(2,1)} %copy-done.14, bf16[8,64,12,32]{1,0,3,2:T(8,128)(2,1)} %reshape.452), kind=kOutput, calls=%fused_computation.7 | convolution fusion | flops 26339328 | bytes 3981312 | tf_op jit(solution)/shard_map/bnqhd,bnkhd->bnhqk/dot_general | solution.py:22
  57.9 0.6 copy-done.4
  58.6 2.2 multiply_reduce_fusion
  60.7 4.3 %fusion.22 = (f32[8,64,12]{1,2,0:T(8,128)S(1)}, f32[8,12,32,64]{3,2,1,0:T(8,128)}) fusion(f32[8,64,12]{1,2,0:T(8,128)S(1)} %add_rsqrt_fusion.1, bf16[1,8,64,1,12,32]{2,1,5,4,3,0:T(8,128)(2,1)S(1)} %get-tuple-element.20, f32[8,12,64,64]{2,3,1,0:T(8,128)S(1)} %get-tuple-element.18, f32[12]{0:T(128)S(1)} %minimum_exponential_fusion, ...), kind=kOutput, calls=%fused_computation.35 | convolution fusion | flops 152561664 | bytes 3219504 | tf_op jit(solution)/shard_map/bnhqk,bnkhd->bnqhd/dot_general | solution.py:26
  65.0 6.8 %fusion.18 = (f32[8,64,12]{1,2,0:T(8,128)}, f32[8,12,32,64]{3,2,1,0:T(8,128)}) fusion(f32[8,64,12]{1,2,0:T(8,128)S(1)} %add_rsqrt_fusion, bf16[1,8,64,1,12,32]{2,1,5,4,3,0:T(8,128)(2,1)S(1)} %get-tuple-element.19, f32[8,12,64,64]{2,3,1,0:T(8,128)S(1)} %get-tuple-element.18, f32[12]{0:T(128)S(1)} %minimum_exponential_fusion, ...), kind=kOutput, calls=%fused_computation.31 | convolution fusion | flops 152561664 | bytes 3219504 | tf_op jit(solution)/shard_map/bnhqk,bnqhd->bnkhd/dot_general | solution.py:26
  71.9 0.9 convolution_bitcast_fusion
  73.1 2.6 %fusion.21 = (bf16[1,8,64,1,12,32]{2,5,4,1,3,0:T(8,128)(2,1)S(1)}, bf16[1,8,64,1,12,32]{2,5,4,1,3,0:T(8,128)(2,1)S(1)}) fusion(f32[8,12,32,64]{3,2,1,0:T(8,128)} %get-tuple-element.31, f32[8,64,12]{1,2,0:T(8,128)} %get-tuple-element.30, f32[8,64,12]{1,2,0:T(8,128)S(1)} %add_rsqrt_fusion, bf16[1,8,64,1,12,32]{2,1,5,4,3,0:T(8,128)(2,1)S(1)} %get-tuple-element.19, ...), kind=kLoop, calls=%fused_computation.34 | loop fusion | flops 2359296 | bytes 3244032 | tf_op jit(solution)/shard_map/stack | solution.py:135
  75.7 0.6 maximum_convert_fusion
  76.3 2.7 %copy.98 = bf16[1,8,64,3,12,32]{2,1,5,4,3,0:T(8,128)(2,1)S(1)} copy(bf16[1,8,64,3,12,32]{2,5,4,1,3,0:T(8,128)(2,1)S(1)} %maximum_convert_fusion) | data formatting | bytes 2359296 | tf_op jit(solution)/shard_map/convert_element_type | solution.py:135
  79.1 2.4 %convert_element_type.207 = bf16[512,1152]{0,1:T(8,128)(2,1)} reshape(bf16[1,8,64,3,12,32]{2,1,5,4,3,0:T(8,128)(2,1)S(1)} %copy.98) | data formatting | bytes 2359296 | tf_op jit(solution)/shard_map/convert_element_type | solution.py:135
  81.5 3.1 %convolution_convert_fusion.1 = bf16[384,1152]{0,1:T(8,128)(2,1)} fusion(bf16[512,1152]{0,1:T(8,128)(2,1)} %convert_element_type.207, bf16[512,384]{1,0:T(8,128)(2,1)} %bitcast.142), kind=kOutput, calls=%fused_computation.15 | convolution fusion | flops 453427200 | bytes 2457600 | tf_op jit(solution)/shard_map/dot_general | solution.py:136
  84.9 0.9 copy-done.11
  85.8 0.9 convolution_convert_fusion.3
  86.8 1.6 collective-permute-start.2
  88.4 1.4 fusion.41
  89.8 1.1 collective-permute-done.2
  91.1 29.3 %all-reduce.1 = (f32[12,225]{1,0:T(8,128)S(1)}, f32[12]{0:T(128)S(1)}, f32[384]{0:T(512)S(1)}) all-reduce(f32[12,225]{1,0:T(8,128)S(1)} %fusion.41, f32[12]{0:T(128)S(1)} %compare_select_fusion.1, f32[384]{0:T(512)S(1)} %get-tuple-element.8), channel_id=1, replica_groups=mesh['ha'=8,'wa'=2,'ba'=2] {'ha'}, use_global_device_ids=true, to_apply=%region_16.17 | all-reduce | flops 3096 | bytes 24768 | tf_op jit(solution)/shard_map/psum | solution.py:183
  120.4 17.0 %all-reduce.2 = (f32[12,225]{1,0:T(8,128)}, f32[12]{0:T(128)}, f32[384]{0:T(512)}) all-reduce(f32[12,225]{1,0:T(8,128)S(1)} %get-tuple-element.12, f32[12]{0:T(128)S(1)} %get-tuple-element.13, f32[384]{0:T(512)S(1)} %get-tuple-element.14), channel_id=1, replica_groups=mesh['ha'=8,'wa'=2,'ba'=2] {'wa','ba'}, use_global_device_ids=true, to_apply=%region_17.18 | all-reduce | flops 3096 | bytes 24768 | tf_op jit(solution)/shard_map/psum | solution.py:183
  137.4 0.9 add_convert_fusion
  138.3 75.2 %all-reduce.4 = (f32[384,576]{0,1:T(8,128)}, f32[384,192]{0,1:T(8,128)}) all-reduce(bf16[384,576]{0,1:T(8,128)(2,1)} %reduce-scatter.3.cloned.1.call-done, bf16[384,192]{0,1:T(8,128)(2,1)} %reduce-scatter.5.cloned.1.call-done), channel_id=1, replica_groups=mesh['ha'=8,'wa'=2,'ba'=2] {'ha','wa'}, use_global_device_ids=true, to_apply=%region_12.13 | all-reduce | flops 294912 | bytes 1769472 | tf_op jit(solution)/shard_map/psum | solution.py:182
  (76 shorter events, 3.8 us)
Async XLA Ops:
  7.2 17.5 %copy-start = (bf16[384,1152]{1,0:T(8,128)(2,1)S(1)}, bf16[384,1152]{1,0:T(8,128)(2,1)}, u32[]{:S(2)}) copy-start(bf16[384,1152]{1,0:T(8,128)(2,1)} %param.9) | copy-start | bytes 2654212
  7.2 8.0 %copy-start.17 = (f32[12,225]{1,0:T(8,128)S(1)}, f32[12,225]{1,0:T(8,128)}, u32[]{:S(2)}) copy-start(f32[12,225]{1,0:T(8,128)} %param.11) | copy-start | bytes 32404
  7.2 131.1 %reduce-scatter.5.cloned.1.call-start = ((), (), s32[]{:S(2)}) async-start(), calls=%async_computation.3 | async-start | bytes 442368 | tf_op jit(solution)/shard_map/reduce_scatter | solution.py:178
  8.3 10.0 %collective-permute-start = (bf16[2,1,4,32,384]{4,3,2,1,0:T(8,128)(2,1)S(1)}, bf16[2,1,4,32,384]{4,3,2,1,0:T(8,128)(2,1)S(1)}, u32[]{:S(2)}, u32[]{:S(2)}) collective-permute-start(bf16[2,1,4,32,384]{4,3,2,1,0:T(8,128)(2,1)S(1)} %pad_maximum_fusion.2), channel_id=1, source_target_pairs={{4,0},{8,4},{12,8},{16,12},{20,16},{24,20},{28,24},{0,28},{5,1},{9... | collective-permute-start | bytes 589832 | tf_op jit(solution)/shard_map/ppermute | solution.py:18
  14.0 4.3 %copy-start.18 = (f32[12]{0:T(128)S(1)}, f32[12]{0:T(128)}, u32[]{:S(2)}) copy-start(f32[12]{0:T(128)} %param.12) | copy-start | bytes 148
  18.3 4.7 %collective-permute-start.1 = (bf16[2,1,16,4,384]{4,3,2,1,0:T(4,128)(2,1)S(1)}, bf16[2,1,16,4,384]{4,3,2,1,0:T(4,128)(2,1)S(1)}, u32[]{:S(2)}, u32[]{:S(2)}) collective-permute-start(bf16[2,1,16,4,384]{4,3,2,1,0:T(4,128)(2,1)S(1)} %pad_maximum_fusion.4), channel_id=1, source_target_pairs={{2,0},{0,2},{3,1},{1,3},{6,4},{4,6},{7,5},{5,7},{10,8},{8,10},{11,... | collective-permute-start | bytes 294920 | tf_op jit(solution)/shard_map/ppermute | solution.py:18
  24.0 0.7 copy-start.9
  30.9 7.7 %copy-start.14 = (bf16[1,8,64,1,12,32]{2,1,5,4,3,0:T(8,128)(2,1)}, bf16[1,8,64,1,12,32]{2,1,5,4,3,0:T(8,128)(2,1)S(1)}, u32[]{:S(2)}) copy-start(bf16[1,8,64,1,12,32]{2,1,5,4,3,0:T(8,128)(2,1)S(1)} %get-tuple-element.21) | copy-start | bytes 1179652
  31.7 5.2 %copy-start.10 = (f32[12,64,64]{1,2,0:T(8,128)S(1)}, f32[12,64,64]{1,2,0:T(8,128)}, u32[]{:S(2)}) copy-start(f32[12,64,64]{1,2,0:T(8,128)} %copy.85) | copy-start | bytes 589828
  31.7 5.2 %copy-start.13 = (f32[8,64,64]{1,2,0:T(8,128)S(1)}, f32[8,64,64]{1,2,0:T(8,128)}, u32[]{:S(2)}) copy-start(f32[8,64,64]{1,2,0:T(8,128)} %compare_select_fusion) | copy-start | bytes 393220
  36.9 1.7 copy-start.1
  38.6 1.7 copy-start.3
  42.1 1.7 copy-start.6
  43.9 3.2 %copy-start.16 = (f32[384]{0:T(512)S(1)}, f32[384]{0:T(512)}, u32[]{:S(2)}) copy-start(f32[384]{0:T(512)} %param.13) | copy-start | bytes 4612
  49.8 1.4 copy-start.12
  49.8 1.9 copy-start.5
  54.3 3.6 %copy-start.2 = (f32[8,12,64,64]{2,3,1,0:T(8,128)S(1)}, f32[8,12,64,64]{2,3,1,0:T(8,128)}, u32[]{:S(2)}) copy-start(f32[8,12,64,64]{2,3,1,0:T(8,128)} %copy-done.1) | copy-start | bytes 4718596
  54.3 4.3 %copy-start.4 = (f32[8,12,64,64]{2,3,1,0:T(8,128)S(1)}, f32[8,12,64,64]{2,3,1,0:T(8,128)}, u32[]{:S(2)}) copy-start(f32[8,12,64,64]{2,3,1,0:T(8,128)} %copy-done.3) | copy-start | bytes 4718596
  65.0 6.8 %copy-start.15 = (bf16[8,64,12,32]{1,0,3,2:T(8,128)(2,1)S(1)}, bf16[8,64,12,32]{1,0,3,2:T(8,128)(2,1)}, u32[]{:S(2)}) copy-start(bf16[8,64,12,32]{1,0,3,2:T(8,128)(2,1)} %reshape.452) | copy-start | bytes 1179652
  72.8 65.4 %reduce-scatter.3.cloned.1.call-start = ((), (), s32[]{:S(2)}) async-start(), calls=%async_computation.2 | async-start | bytes 1327104 | tf_op jit(solution)/shard_map/reduce_scatter | solution.py:175
  81.5 3.1 %copy-start.8 = (f32[12,64,64]{1,2,0:T(8,128)S(1)}, f32[12,64,64]{1,2,0:T(8,128)}, u32[]{:S(2)}) copy-start(f32[12,64,64]{1,2,0:T(8,128)} %get-tuple-element.7) | copy-start | bytes 589828
  84.6 1.3 copy-start.11
  86.7 50.7 %copy-start.7 = (bf16[1,16,32,384]{3,2,1,0:T(8,128)(2,1)S(1)}, bf16[1,16,32,384]{3,2,1,0:T(8,128)(2,1)}, u32[]{:S(2)}) copy-start(bf16[1,16,32,384]{3,2,1,0:T(8,128)(2,1)} %param.8) | copy-start | bytes 1179652
  86.8 4.2 %collective-permute-start.2 = (bf16[1,16,4,384]{3,2,1,0:T(4,128)(2,1)S(1)}, bf16[1,16,4,384]{3,2,1,0:T(4,128)(2,1)S(1)}, u32[]{:S(2)}, u32[]{:S(2)}) collective-permute-start(bf16[1,16,4,384]{3,2,1,0:T(4,128)(2,1)S(1)} %slice.61), channel_id=1, source_target_pairs={{2,0},{0,2},{3,1},{1,3},{6,4},{4,6},{7,5},{5,7},{10,8},{8,10},{11,... | collective-permute-start | bytes 147464 | tf_op jit(solution)/shard_map/ppermute | solution.py:18
  91.0 46.4 %collective-permute-start.3 = (bf16[1,4,32,384]{3,2,1,0:T(8,128)(2,1)S(1)}, bf16[1,4,32,384]{3,2,1,0:T(8,128)(2,1)S(1)}, u32[]{:S(2)}, u32[]{:S(2)}) collective-permute-start(bf16[1,4,32,384]{3,2,1,0:T(8,128)(2,1)S(1)} %pad_maximum_fusion.3), channel_id=1, source_target_pairs={{28,0},{0,4},{4,8},{8,12},{12,16},{16,20},{20,24},{24,28},{29,1},{... | collective-permute-start | bytes 294920 | tf_op jit(solution)/shard_map/ppermute | solution.py:18
Sparse Core Ops, SparseCore 0:
  73.0 11.1 reduce-scatter.4
  87.0 18.5 reduce-scatter.2
